TPU v7x, 256 devices: a whole 4x4x8 slice. The times are simulated.
256 devices in a mesh: gy: 16 (over x_hi, y, core), gx: 16 (over x_lo, z).
Axes of the slice: x: 4 (x_hi: 2, x_lo: 2; x = x_hi * 2 + x_lo), y: 4, z: 8, core: 2. Of those that a mesh axis runs over, the one named last changes fastest.
Arguments:
- feat_a: float32 [1024, 1024, 128], P('gy', 'gx'), may hold values from -8 to 8
- feat_b: float32 [1024, 1024, 128], P('gy', 'gx'), may hold values from -8 to 8
- occ_a: int32 [1024, 1024], P('gy', 'gx'), may hold values from 0 to 1, as said below
- occ_b: int32 [1024, 1024], P('gy', 'gx'), may hold values from 0 to 1, as said below
- first_weight: bfloat16 [256, 256], replicated, may hold values from -0.375 to 0.375
- second_weight: bfloat16 [256, 128], replicated, may hold values from -0.375 to 0.375
Outputs:
- matched_a: float32 [1024, 1024, 128], P('gy', 'gx')
- matched_b: float32 [1024, 1024, 128], P('gy', 'gx')
Inputs may be any that keep to these rules, and one draw needn't show every extreme that they name: `occ_a`: 1 marks an occupied cell. `occ_b`: 1 marks an occupied cell.
All inputs are finite; a program needn't handle non-finite values.
Results may differ from a plain program's by a relative error of at most 0.0042.
Values may be sent and summed in bfloat16 or wider, within the bound.
No kernel may reach another device: no remote copies, remote signals or barrier semaphores. Data moves between devices by JAX's collectives and lax.ppermute only.
A program may use at most 64 MiB of HBM per device.

v0:
```python
import functools

import jax
import jax.numpy as jnp
from jax import lax
from jax.experimental import pallas as pl
from jax.experimental.pallas import tpu as pltpu
from jax.sharding import PartitionSpec as P

R = 8
T = 16
SENT = 2.0**120
LIMIT = 2.0**110
BIG = 2.0**100
LOG2E = 1.4426950408889634
RSQRT2 = 0.7071067811865476


def key_bias(first_row, col_group):
    cell = lax.broadcasted_iota(jnp.int32, (128, 128), 0)
    lane = lax.broadcasted_iota(jnp.int32, (128, 128), 1)
    row = first_row + cell // T
    col = col_group * T + cell % T
    place = jnp.where(lane < 32, row, col)
    inside = ((place - lane) & 31) <= 2 * R
    return jnp.where((lane >= 64) | inside, 0.0, -BIG)


def query_code(ty, tx):
    cell = lax.broadcasted_iota(jnp.int32, (256, 128), 0)
    lane = lax.broadcasted_iota(jnp.int32, (256, 128), 1)
    row = (ty * T + cell // T) & 31
    col = (tx * T + cell % T) & 31
    hit = (lane == row) | (lane == col + 32) | (lane == 64)
    return jnp.where(hit, 1.0, 0.0).astype(jnp.bfloat16)


def assemble(centers, top, bottom, left, right, kc, ke, vt, pc):
    for s in range(2):

        def group(rg, row_of):
            for r in range(8):
                row = rg * 8 + r
                line = jnp.concatenate(
                    [left[s, row], row_of(row, r), right[s, row]], axis=0
                )
                for cg in range(5):
                    kc[s, rg, cg, r * T : (r + 1) * T, :] = line[cg * T : (cg + 1) * T]
            for cg in range(5):
                raw = kc[s, rg, cg].astype(jnp.float32)
                free = raw > LIMIT
                clean = jnp.where(free, 0.0, raw).astype(jnp.bfloat16)
                kc[s, rg, cg] = clean
                vt[s, rg, cg] = clean.T
                ke[s, rg, cg] = jnp.where(free, -BIG, key_bias(rg * 8, cg)).astype(
                    jnp.bfloat16
                )

        group(0, lambda row, r: top[s, r])
        group(9, lambda row, r: bottom[s, r])

        def step(rg, carry):
            group(rg, lambda row, r: centers[s][row - 8])
            return carry

        lax.fori_loop(1, 9, step, 0)
        for h in range(2):
            n = 768 * (1 - h)
            pc[s, n : n + 256, h * 128 : h * 128 + 128] = jnp.zeros((256, 128), jnp.bfloat16)


def kernel(emit, tiles, ca, cb, top, bottom, left, right, fa, fb, w1, w2, *rest):
    keyed = (None, None)
    if emit:
        oa, ob, *rest = rest
        keyed = (rest[0], rest[1])
        rest = rest[2:]
    else:
        oa, ob, *rest = rest
    kc, ke, vt, sc, pc, ct, mx, sm = rest
    centers = (ca, cb)
    feats = (fa, fb)
    outs = (oa, ob)
    across = tiles[1]
    last = tiles[0] * tiles[1] - 1
    scale = LOG2E / 128.0**0.5
    j = pl.program_id(0)

    def place(t):
        t = jnp.clip(t, 0, last)
        return t // across, t % across

    def tile_of(s, ty, tx):
        raw = centers[s][pl.ds(ty * T, T), pl.ds(pl.multiple_of(tx * T, T), T), :]
        raw = raw.reshape(256, 128).astype(jnp.float32)
        free = raw > LIMIT
        return free, jnp.where(free, 0.0, raw).astype(jnp.bfloat16)

    def score(s, t):
        ty, tx = place(t)
        k = 1 - s
        unused, query = tile_of(s, ty, tx)
        full = jnp.concatenate([query, query_code(ty, tx)], axis=1)
        best = [None, None]
        for i in range(2):
            rows = pl.ds(2 * ty + 2 * i, 2)
            cols = pl.ds(tx, 2)
            keys = jnp.concatenate(
                [
                    kc[k, rows, cols].reshape(512, 128),
                    ke[k, rows, cols].reshape(512, 128),
                ],
                axis=1,
            )
            scores = lax.dot_general(
                keys, full, (((1,), (1,)), ((), ())), preferred_element_type=jnp.float32
            )
            for h in range(2):
                lo, hi = max(256 * h, 512 * i), min(256 * h + 768, 512 * i + 512)
                part = scores[lo - 512 * i : hi - 512 * i, h * 128 : h * 128 + 128]
                sc[s, lo:hi, h * 128 : h * 128 + 128] = part
                top_now = part.reshape((hi - lo) // 8, 8, 128).max(0)
                best[h] = top_now if best[h] is None else jnp.maximum(best[h], top_now)
            yield
        for h in range(2):
            mx[s, :, h * 128 : h * 128 + 128] = best[h]
        yield

    def weigh(s):
        for h in range(2):
            lanes = slice(h * 128, h * 128 + 128)
            best = jnp.maximum(mx[s, :, lanes].max(0, keepdims=True), 0.0)
            total = jnp.zeros((8, 128), jnp.float32)
            for n in range(256 * h, 256 * h + 768, 128):
                e = jnp.exp2((sc[s, n : n + 128, lanes] - best) * scale)
                total = total + e.reshape(16, 8, 128).sum(0)
                pc[s, n : n + 128, lanes] = e.astype(jnp.bfloat16)
                if (n - 256 * h) % 256 == 128:
                    yield
            total = total.sum(0, keepdims=True) + jnp.exp2(-best * scale)
            sm[s, :, lanes] = jnp.broadcast_to(1.0 / total, (8, 128))
        yield

    def gather(s, t):
        ty, tx = place(t)
        k = 1 - s
        values = jnp.concatenate(
            [vt[k, 2 * ty + i, tx + c] for i in range(4) for c in range(2)], axis=1
        )
        carried = jnp.dot(values, pc[s], preferred_element_type=jnp.float32)
        ct[s] = (carried * sm[s][:1]).astype(jnp.bfloat16)
        yield

    def update(s, t):
        ty, tx = place(t)
        free, query = tile_of(s, ty, tx)
        joined = jnp.concatenate([query, ct[s].T], axis=1)
        x = jnp.dot(joined, w1[...], preferred_element_type=jnp.float32)
        hidden = (0.5 * x * (1.0 + lax.erf(x * RSQRT2))).astype(jnp.bfloat16)
        yield
        change = jnp.dot(hidden, w2[...], preferred_element_type=jnp.float32)
        old = feats[s][...].reshape(256, 128)
        new = jnp.where(free, old, old + change)
        outs[s][...] = new.reshape(T, T, 128)
        if emit:
            keyed[s][...] = jnp.where(free, SENT, new).astype(jnp.bfloat16).reshape(T, T, 128)
        yield

    @pl.when(j == 0)
    def _():
        assemble(centers, top, bottom, left, right, kc, ke, vt, pc)
        for unused in score(0, 0):
            pass

    for stages in (
        (update(1, j - 2), gather(1, j - 1), score(1, j), weigh(0)),
        (update(0, j - 1), gather(0, j), score(0, j + 1), weigh(1)),
    ):
        stages = list(stages)
        while stages:
            stages = [stage for stage in stages if next(stage, True) is None]


def one_pass(emit, centers, rims, feat_a, feat_b, first_weight, second_weight):
    rows, cols, channels = feat_a.shape
    tiles = (rows // T, cols // T)
    count = tiles[0] * tiles[1]
    whole = pl.BlockSpec(memory_space=pltpu.VMEM)

    def tile(delay):
        def at(j):
            t = jnp.clip(j - delay, 0, count - 1)
            return t // tiles[1], t % tiles[1], 0

        return pl.BlockSpec((T, T, channels), at)

    out_shape = [jax.ShapeDtypeStruct(feat_a.shape, jnp.float32)] * 2
    out_specs = [tile(1), tile(2)]
    if emit:
        out_shape += [jax.ShapeDtypeStruct(feat_a.shape, jnp.bfloat16)] * 2
        out_specs += [tile(1), tile(2)]
    blocks = (2, (rows + 2 * R) // 8, (cols + 2 * R) // T, 128, 128)
    flops = 2 * 16 * (2 * 1024 * 256 * 256 * 2 + 256 * 256 * 384 * 2)
    return pl.pallas_call(
        functools.partial(kernel, emit, tiles),
        grid=(count + 2,),
        in_specs=[whole] * 6 + [tile(1), tile(2), whole, whole],
        out_specs=out_specs,
        out_shape=out_shape,
        scratch_shapes=[
            pltpu.VMEM(blocks, jnp.bfloat16),
            pltpu.VMEM(blocks, jnp.bfloat16),
            pltpu.VMEM(blocks, jnp.bfloat16),
            pltpu.VMEM((2, 1024, 256), jnp.float32),
            pltpu.VMEM((2, 1024, 256), jnp.bfloat16),
            pltpu.VMEM((2, 128, 256), jnp.bfloat16),
            pltpu.VMEM((2, 8, 256), jnp.float32),
            pltpu.VMEM((2, 8, 256), jnp.float32),
        ],
        compiler_params=pltpu.CompilerParams(
            dimension_semantics=("arbitrary",), vmem_limit_bytes=44 << 20
        ),
        cost_estimate=pl.CostEstimate(
            flops=flops, bytes_accessed=14 << 20, transcendentals=2 * 16 * 768 * 256
        ),
        name="match_pass",
    )(*centers, *rims, feat_a, feat_b, first_weight, second_weight)


def shifted(cells, axis, up):
    count = lax.axis_size(axis)
    me = lax.axis_index(axis)
    if up:
        pairs = [(i, i + 1) for i in range(count - 1)]
        edge = me == 0
    else:
        pairs = [(i + 1, i) for i in range(count - 1)]
        edge = me == count - 1
    got = lax.ppermute(cells, axis, pairs)
    return jnp.where(edge, jnp.asarray(SENT, got.dtype), got)


def exchange(centers):
    def both(rows, cols):
        return jnp.stack([center[rows, cols] for center in centers])

    near, far, all_cells = slice(0, R), slice(-R, None), slice(None)
    top = shifted(both(far, all_cells), "gy", True)
    bottom = shifted(both(near, all_cells), "gy", False)
    head, tail = (
        jnp.concatenate([top[:, :, side], both(all_cells, side), bottom[:, :, side]], axis=1)
        for side in (near, far)
    )
    left = shifted(tail, "gx", True)
    right = shifted(head, "gx", False)
    return top, bottom, left, right


def local(feat_a, feat_b, occ_a, occ_b, first_weight, second_weight):
    centers = [
        jnp.where(occ[..., None] > 0, feat, SENT).astype(jnp.bfloat16)
        for feat, occ in ((feat_a, occ_a), (feat_b, occ_b))
    ]
    feat_a, feat_b, *centers = one_pass(
        True, centers, exchange(centers), feat_a, feat_b, first_weight, second_weight
    )
    return tuple(
        one_pass(False, centers, exchange(centers), feat_a, feat_b, first_weight, second_weight)
    )


def solution(mesh):
    in_specs = (P("gy", "gx", None), P("gy", "gx", None), P("gy", "gx"), P("gy", "gx"), P(), P())
    out_specs = (P("gy", "gx", None), P("gy", "gx", None))
    return jax.shard_map(local, mesh=mesh, in_specs=in_specs, out_specs=out_specs, check_vma=False)
```

profile of v0, /device:TPU:57, one launch (start us, length us, event | category | flops | bytes accessed | tf_op | source)
XLA Modules:
  0.0 113.4 jit_solution(14976992198221013769)
XLA Ops:
  0.6 0.9 broadcast_compare_fusion.1
  1.6 0.8 broadcast_compare_fusion
  2.3 1.9 %select_convert_fusion.cb = bf16[64,64,128]{2,1,0:T(8,128)(2,1)S(1)} fusion(f32[64,64,128]{2,1,0:T(8,128)} %fb.1, pred[64,64]{1,0:T(8,128)(4,1)S(1)} %broadcast_compare_fusion), kind=kLoop, calls=%fused_computation | loop fusion | flops 524288 | bytes 3149824 | tf_op jit(solution)/shard_map/convert_element_type | solution.py:261
  4.3 0.7 select_convert_fusion.1.ca
  5.1 4.9 %collective-permute-start = (bf16[2,8,64,128]{3,2,1,0:T(8,128)(2,1)S(1)}, bf16[2,8,64,128]{3,2,1,0:T(8,128)(2,1)S(1)}, u32[]{:S(2)}, u32[]{:S(2)}) collective-permute-start(bf16[2,8,64,128]{3,2,1,0:T(8,128)(2,1)S(1)} %pad_maximum_fusion.4), channel_id=1, source_target_pairs={{0,16},{16,32},{32,48},{48,64},{64,80},{80,96},{96,112},{112,128},... | collective-permute-start | bytes 786440 | tf_op jit(solution)/shard_map/ppermute | solution.py:239
  10.0 1.9 %collective-permute-start.1 = (bf16[2,8,64,128]{3,2,1,0:T(8,128)(2,1)S(1)}, bf16[2,8,64,128]{3,2,1,0:T(8,128)(2,1)S(1)}, u32[]{:S(2)}, u32[]{:S(2)}) collective-permute-start(bf16[2,8,64,128]{3,2,1,0:T(8,128)(2,1)S(1)} %pad_maximum_fusion.5), channel_id=1, source_target_pairs={{16,0},{32,16},{48,32},{64,48},{80,64},{96,80},{112,96},{128,112},... | collective-permute-start | bytes 786440 | tf_op jit(solution)/shard_map/ppermute | solution.py:239
  12.1 1.2 %collective-permute-done = bf16[2,8,64,128]{3,2,1,0:T(8,128)(2,1)S(1)} collective-permute-done((bf16[2,8,64,128]{3,2,1,0:T(8,128)(2,1)S(1)}, bf16[2,8,64,128]{3,2,1,0:T(8,128)(2,1)S(1)}, u32[]{:S(2)}, u32[]{:S(2)}) %collective-permute-start) | collective-permute-done | bytes 262176 | tf_op jit(solution)/shard_map/ppermute | solution.py:239
  13.3 8.0 %collective-permute-done.1 = bf16[2,8,64,128]{3,2,1,0:T(8,128)(2,1)S(1)} collective-permute-done((bf16[2,8,64,128]{3,2,1,0:T(8,128)(2,1)S(1)}, bf16[2,8,64,128]{3,2,1,0:T(8,128)(2,1)S(1)}, u32[]{:S(2)}, u32[]{:S(2)}) %collective-permute-start.1) | collective-permute-done | bytes 262176 | tf_op jit(solution)/shard_map/ppermute | solution.py:239
  21.4 3.5 %collective-permute-start.2 = (bf16[2,80,8,128]{3,2,1,0:T(8,128)(2,1)S(1)}, bf16[2,80,8,128]{3,2,1,0:T(8,128)(2,1)}, u32[]{:S(2)}, u32[]{:S(2)}) collective-permute-start(bf16[2,80,8,128]{3,2,1,0:T(8,128)(2,1)S(1)} %pad_maximum_fusion), channel_id=1, source_target_pairs={{0,1},{1,2},{2,3},{3,4},{4,5},{5,6},{6,7},{7,8},{8,9},{9,10},{10,1... | collective-permute-start | bytes 983048 | tf_op jit(solution)/shard_map/ppermute | solution.py:239
  25.0 2.5 %collective-permute-start.3 = (bf16[2,80,8,128]{3,2,1,0:T(8,128)(2,1)S(1)}, bf16[2,80,8,128]{3,2,1,0:T(8,128)(2,1)}, u32[]{:S(2)}, u32[]{:S(2)}) collective-permute-start(bf16[2,80,8,128]{3,2,1,0:T(8,128)(2,1)S(1)} %pad_maximum_fusion.1), channel_id=1, source_target_pairs={{1,0},{2,1},{3,2},{4,3},{5,4},{6,5},{7,6},{8,7},{9,8},{10,9},{11,1... | collective-permute-start | bytes 983048 | tf_op jit(solution)/shard_map/ppermute | solution.py:239
  27.5 1.8 %collective-permute-done.2 = bf16[2,80,8,128]{3,2,1,0:T(8,128)(2,1)} collective-permute-done((bf16[2,80,8,128]{3,2,1,0:T(8,128)(2,1)S(1)}, bf16[2,80,8,128]{3,2,1,0:T(8,128)(2,1)}, u32[]{:S(2)}, u32[]{:S(2)}) %collective-permute-start.2) | collective-permute-done | bytes 327712 | tf_op jit(solution)/shard_map/ppermute | solution.py:239
  29.3 1.0 broadcast_select_fusion.3.left
  30.4 2.8 %collective-permute-done.3 = bf16[2,80,8,128]{3,2,1,0:T(8,128)(2,1)} collective-permute-done((bf16[2,80,8,128]{3,2,1,0:T(8,128)(2,1)S(1)}, bf16[2,80,8,128]{3,2,1,0:T(8,128)(2,1)}, u32[]{:S(2)}, u32[]{:S(2)}) %collective-permute-start.3) | collective-permute-done | bytes 327712 | tf_op jit(solution)/shard_map/ppermute | solution.py:239
  33.1 1.0 broadcast_select_fusion.1.right
  34.2 25.2 %match_pass.2 = (f32[64,64,128]{2,1,0:T(8,128)S(1)}, f32[64,64,128]{2,1,0:T(8,128)S(1)}, bf16[64,64,128]{2,1,0:T(8,128)(2,1)S(1)}, bf16[64,64,128]{2,1,0:T(8,128)(2,1)S(1)}) custom-call(bf16[64,64,128]{2,1,0:T(8,128)(2,1)S(1)} %select_convert_fusion.1.ca, bf16[64,64,128]{2,1,0:T(8,128)(2,1)S(1)} %select_convert_fusion.cb, ...), custom_call_target="tpu_custom_call" | custom-call | flops 10200547328 | bytes 14680064 | tf_op jit(solution)/shard_map/match_pass/pallas_call | solution.py:204
  59.5 3.8 %collective-permute-start.4 = (bf16[2,8,64,128]{3,2,1,0:T(8,128)(2,1)S(1)}, bf16[2,8,64,128]{3,2,1,0:T(8,128)(2,1)S(1)}, u32[]{:S(2)}, u32[]{:S(2)}) collective-permute-start(bf16[2,8,64,128]{3,2,1,0:T(8,128)(2,1)S(1)} %pad_maximum_fusion.6), channel_id=1, source_target_pairs={{0,16},{16,32},{32,48},{48,64},{64,80},{80,96},{96,112},{112,128},... | collective-permute-start | bytes 786440 | tf_op jit(solution)/shard_map/ppermute | solution.py:239
  63.3 1.9 %collective-permute-start.5 = (bf16[2,8,64,128]{3,2,1,0:T(8,128)(2,1)S(1)}, bf16[2,8,64,128]{3,2,1,0:T(8,128)(2,1)S(1)}, u32[]{:S(2)}, u32[]{:S(2)}) collective-permute-start(bf16[2,8,64,128]{3,2,1,0:T(8,128)(2,1)S(1)} %pad_maximum_fusion.7), channel_id=1, source_target_pairs={{16,0},{32,16},{48,32},{64,48},{80,64},{96,80},{112,96},{128,112},... | collective-permute-start | bytes 786440 | tf_op jit(solution)/shard_map/ppermute | solution.py:239
  65.3 1.3 %collective-permute-done.4 = bf16[2,8,64,128]{3,2,1,0:T(8,128)(2,1)S(1)} collective-permute-done((bf16[2,8,64,128]{3,2,1,0:T(8,128)(2,1)S(1)}, bf16[2,8,64,128]{3,2,1,0:T(8,128)(2,1)S(1)}, u32[]{:S(2)}, u32[]{:S(2)}) %collective-permute-start.4) | collective-permute-done | bytes 262176 | tf_op jit(solution)/shard_map/ppermute | solution.py:239
  66.6 8.0 %collective-permute-done.5 = bf16[2,8,64,128]{3,2,1,0:T(8,128)(2,1)S(1)} collective-permute-done((bf16[2,8,64,128]{3,2,1,0:T(8,128)(2,1)S(1)}, bf16[2,8,64,128]{3,2,1,0:T(8,128)(2,1)S(1)}, u32[]{:S(2)}, u32[]{:S(2)}) %collective-permute-start.5) | collective-permute-done | bytes 262176 | tf_op jit(solution)/shard_map/ppermute | solution.py:239
  74.7 4.8 %collective-permute-start.6 = (bf16[2,80,8,128]{3,2,1,0:T(8,128)(2,1)S(1)}, bf16[2,80,8,128]{3,2,1,0:T(8,128)(2,1)S(1)}, u32[]{:S(2)}, u32[]{:S(2)}) collective-permute-start(bf16[2,80,8,128]{3,2,1,0:T(8,128)(2,1)S(1)} %pad_maximum_fusion.2), channel_id=1, source_target_pairs={{0,1},{1,2},{2,3},{3,4},{4,5},{5,6},{6,7},{7,8},{8,9},{9,10},{10,1... | collective-permute-start | bytes 983048 | tf_op jit(solution)/shard_map/ppermute | solution.py:239
  79.6 1.9 %collective-permute-start.7 = (bf16[2,80,8,128]{3,2,1,0:T(8,128)(2,1)S(1)}, bf16[2,80,8,128]{3,2,1,0:T(8,128)(2,1)S(1)}, u32[]{:S(2)}, u32[]{:S(2)}) collective-permute-start(bf16[2,80,8,128]{3,2,1,0:T(8,128)(2,1)S(1)} %pad_maximum_fusion.3), channel_id=1, source_target_pairs={{1,0},{2,1},{3,2},{4,3},{5,4},{6,5},{7,6},{8,7},{9,8},{10,9},{11,1... | collective-permute-start | bytes 983048 | tf_op jit(solution)/shard_map/ppermute | solution.py:239
  81.5 2.0 %collective-permute-done.6 = bf16[2,80,8,128]{3,2,1,0:T(8,128)(2,1)S(1)} collective-permute-done((bf16[2,80,8,128]{3,2,1,0:T(8,128)(2,1)S(1)}, bf16[2,80,8,128]{3,2,1,0:T(8,128)(2,1)S(1)}, u32[]{:S(2)}, u32[]{:S(2)}) %collective-permute-start.6) | collective-permute-done | bytes 327712 | tf_op jit(solution)/shard_map/ppermute | solution.py:239
  83.5 5.1 %collective-permute-done.7 = bf16[2,80,8,128]{3,2,1,0:T(8,128)(2,1)S(1)} collective-permute-done((bf16[2,80,8,128]{3,2,1,0:T(8,128)(2,1)S(1)}, bf16[2,80,8,128]{3,2,1,0:T(8,128)(2,1)S(1)}, u32[]{:S(2)}, u32[]{:S(2)}) %collective-permute-start.7) | collective-permute-done | bytes 327712 | tf_op jit(solution)/shard_map/ppermute | solution.py:239
  88.7 24.8 %match_pass.3 = (f32[64,64,128]{2,1,0:T(8,128)}, f32[64,64,128]{2,1,0:T(8,128)}) custom-call(bf16[64,64,128]{2,1,0:T(8,128)(2,1)S(1)} %get-tuple-element.6.ca, bf16[64,64,128]{2,1,0:T(8,128)(2,1)S(1)} %get-tuple-element.7.cb, bf16[2,8,64,128]{3,2,1,0:T(8,128)(2,1)S(1)} %broadcast_select_fusion.6.top, ...), custom_call_target="tpu_custom_call" | custom-call | flops 10200547328 | bytes 14680064 | tf_op jit(solution)/shard_map/match_pass/pallas_call | solution.py:204
  (30 shorter events, 0.8 us)
Async XLA Ops:
  0.6 3.6 %copy-start.2 = (f32[64,64,128]{2,1,0:T(8,128)S(1)}, f32[64,64,128]{2,1,0:T(8,128)}, u32[]{:S(2)}) copy-start(f32[64,64,128]{2,1,0:T(8,128)} %fa.1) | copy-start | bytes 6291460
  5.1 8.2 %collective-permute-start = (bf16[2,8,64,128]{3,2,1,0:T(8,128)(2,1)S(1)}, bf16[2,8,64,128]{3,2,1,0:T(8,128)(2,1)S(1)}, u32[]{:S(2)}, u32[]{:S(2)}) collective-permute-start(bf16[2,8,64,128]{3,2,1,0:T(8,128)(2,1)S(1)} %pad_maximum_fusion.4), channel_id=1, source_target_pairs={{0,16},{16,32},{32,48},{48,64},{64,80},{80,96},{96,112},{112,128},... | collective-permute-start | bytes 786440 | tf_op jit(solution)/shard_map/ppermute | solution.py:239
  10.0 11.3 %collective-permute-start.1 = (bf16[2,8,64,128]{3,2,1,0:T(8,128)(2,1)S(1)}, bf16[2,8,64,128]{3,2,1,0:T(8,128)(2,1)S(1)}, u32[]{:S(2)}, u32[]{:S(2)}) collective-permute-start(bf16[2,8,64,128]{3,2,1,0:T(8,128)(2,1)S(1)} %pad_maximum_fusion.5), channel_id=1, source_target_pairs={{16,0},{32,16},{48,32},{64,48},{80,64},{96,80},{112,96},{128,112},... | collective-permute-start | bytes 786440 | tf_op jit(solution)/shard_map/ppermute | solution.py:239
  12.0 22.1 %copy-start = (bf16[256,256]{1,0:T(8,128)(2,1)S(1)}, bf16[256,256]{1,0:T(8,128)(2,1)}, u32[]{:S(2)}) copy-start(bf16[256,256]{1,0:T(8,128)(2,1)} %w1.3) | copy-start | bytes 393220
  12.1 22.1 %copy-start.1 = (bf16[256,128]{1,0:T(8,128)(2,1)S(1)}, bf16[256,128]{1,0:T(8,128)(2,1)}, u32[]{:S(2)}) copy-start(bf16[256,128]{1,0:T(8,128)(2,1)} %w2.3) | copy-start | bytes 196612
  21.4 7.9 %collective-permute-start.2 = (bf16[2,80,8,128]{3,2,1,0:T(8,128)(2,1)S(1)}, bf16[2,80,8,128]{3,2,1,0:T(8,128)(2,1)}, u32[]{:S(2)}, u32[]{:S(2)}) collective-permute-start(bf16[2,80,8,128]{3,2,1,0:T(8,128)(2,1)S(1)} %pad_maximum_fusion), channel_id=1, source_target_pairs={{0,1},{1,2},{2,3},{3,4},{4,5},{5,6},{6,7},{7,8},{8,9},{9,10},{10,1... | collective-permute-start | bytes 983048 | tf_op jit(solution)/shard_map/ppermute | solution.py:239
  25.0 8.1 %collective-permute-start.3 = (bf16[2,80,8,128]{3,2,1,0:T(8,128)(2,1)S(1)}, bf16[2,80,8,128]{3,2,1,0:T(8,128)(2,1)}, u32[]{:S(2)}, u32[]{:S(2)}) collective-permute-start(bf16[2,80,8,128]{3,2,1,0:T(8,128)(2,1)S(1)} %pad_maximum_fusion.1), channel_id=1, source_target_pairs={{1,0},{2,1},{3,2},{4,3},{5,4},{6,5},{7,6},{8,7},{9,8},{10,9},{11,1... | collective-permute-start | bytes 983048 | tf_op jit(solution)/shard_map/ppermute | solution.py:239
  59.5 7.1 %collective-permute-start.4 = (bf16[2,8,64,128]{3,2,1,0:T(8,128)(2,1)S(1)}, bf16[2,8,64,128]{3,2,1,0:T(8,128)(2,1)S(1)}, u32[]{:S(2)}, u32[]{:S(2)}) collective-permute-start(bf16[2,8,64,128]{3,2,1,0:T(8,128)(2,1)S(1)} %pad_maximum_fusion.6), channel_id=1, source_target_pairs={{0,16},{16,32},{32,48},{48,64},{64,80},{80,96},{96,112},{112,128},... | collective-permute-start | bytes 786440 | tf_op jit(solution)/shard_map/ppermute | solution.py:239
  63.3 11.3 %collective-permute-start.5 = (bf16[2,8,64,128]{3,2,1,0:T(8,128)(2,1)S(1)}, bf16[2,8,64,128]{3,2,1,0:T(8,128)(2,1)S(1)}, u32[]{:S(2)}, u32[]{:S(2)}) collective-permute-start(bf16[2,8,64,128]{3,2,1,0:T(8,128)(2,1)S(1)} %pad_maximum_fusion.7), channel_id=1, source_target_pairs={{16,0},{32,16},{48,32},{64,48},{80,64},{96,80},{112,96},{128,112},... | collective-permute-start | bytes 786440 | tf_op jit(solution)/shard_map/ppermute | solution.py:239
  74.7 8.8 %collective-permute-start.6 = (bf16[2,80,8,128]{3,2,1,0:T(8,128)(2,1)S(1)}, bf16[2,80,8,128]{3,2,1,0:T(8,128)(2,1)S(1)}, u32[]{:S(2)}, u32[]{:S(2)}) collective-permute-start(bf16[2,80,8,128]{3,2,1,0:T(8,128)(2,1)S(1)} %pad_maximum_fusion.2), channel_id=1, source_target_pairs={{0,1},{1,2},{2,3},{3,4},{4,5},{5,6},{6,7},{7,8},{8,9},{9,10},{10,1... | collective-permute-start | bytes 983048 | tf_op jit(solution)/shard_map/ppermute | solution.py:239
  79.6 9.0 %collective-permute-start.7 = (bf16[2,80,8,128]{3,2,1,0:T(8,128)(2,1)S(1)}, bf16[2,80,8,128]{3,2,1,0:T(8,128)(2,1)S(1)}, u32[]{:S(2)}, u32[]{:S(2)}) collective-permute-start(bf16[2,80,8,128]{3,2,1,0:T(8,128)(2,1)S(1)} %pad_maximum_fusion.3), channel_id=1, source_target_pairs={{1,0},{2,1},{3,2},{4,3},{5,4},{6,5},{7,6},{8,7},{9,8},{10,9},{11,1... | collective-permute-start | bytes 983048 | tf_op jit(solution)/shard_map/ppermute | solution.py:239
where the time goes:
time: 114 us; the launch traced here: 113 us
  Pallas kernels  50 us (44%)
  waiting for transfers between devices  30.2 us (26%)
  starting transfers between devices  25.2 us (22%)
  other arithmetic  6.84 us (6%)
    pallas_call x2, Pallas kernels, one_pass(): pl.pallas_call(functools.partial(kernel, emit, tiles), grid=(count + 2,),...  50 us
    ppermute x8, waiting for transfers between devices, shifted(): got = lax.ppermute(cells, axis, pairs)  30.2 us
    ppermute x8, starting transfers between devices, shifted(): got = lax.ppermute(cells, axis, pairs)  25.2 us
    convert_element_type x2, other arithmetic, local(): jnp.where(occ[..., None] > 0, feat, SENT).astype(jnp.bfloat16)  2.66 us
  transfers between devices with their start and end apart: 8, of which 8 were waited for; matrix products, arithmetic and copies ran while one was open for 1% of the time, Pallas kernels for 0%

commit v1 on v0

v1 whole, which is shorter than its diff:
```python
import functools

import jax
import jax.numpy as jnp
from jax import lax
from jax.experimental import pallas as pl
from jax.experimental.pallas import tpu as pltpu
from jax.sharding import PartitionSpec as P


R = 8
T = 16
SENT = 2.0**120
LIMIT = 2.0**110
BIG = 2.0**100
LOG2E = 1.4426950408889634
RSQRT2 = 0.7071067811865476


def tables():
    lane = jnp.arange(128)

    def spot(shape, width):
        at = jnp.arange(width)
        row = (jnp.arange(shape[0])[:, None, None] * (width // T) + at[:, None] // T) & 31
        col = (jnp.arange(shape[1])[:, None, None] * T + at[:, None] % T) & 31
        return row[:, None], col[None]

    row, col = spot((4, 2), 128)
    inside = ((jnp.where(lane < 32, row, col) - lane) & 31) <= 2 * R
    bias = jnp.where((lane >= 64) | inside, 0.0, -BIG).astype(jnp.bfloat16)
    row, col = spot((2, 2), 256)
    hit = (lane == row) | (lane == col + 32) | (lane == 64)
    return bias, jnp.where(hit, 1.0, 0.0).astype(jnp.bfloat16)


def assemble(centers, top, bottom, left, right, corners, bias, kc, ke, vt, pc):
    sent = jnp.asarray(SENT, jnp.bfloat16)

    def group(s, rg, row_of, left_of, right_of):
        lines = [
            jnp.concatenate([left_of(r), row_of(r), right_of(r)], axis=0) for r in range(8)
        ]
        for cg in range(5):
            raw = jnp.concatenate([line[cg * T : (cg + 1) * T] for line in lines], axis=0)
            free = raw == sent
            clean = jnp.where(free, jnp.zeros_like(raw), raw)
            kc[s, rg, cg] = clean
            vt[s, rg, cg] = clean.T
            ke[s, rg, cg] = jnp.where(free, jnp.full_like(raw, -BIG), bias[rg & 3, cg & 1])

    for s in range(2):
        for rg, source, first in ((0, top, 0), (9, bottom, R)):
            group(
                s,
                rg,
                lambda r: source[s, r],
                lambda r: corners[0][s, first + r],
                lambda r: corners[1][s, first + r],
            )

    def step(rg, carry):
        row = (rg - 1) * 8
        for s in range(2):
            group(
                s,
                rg,
                lambda r: centers[s][row + r],
                lambda r: left[s, row + r],
                lambda r: right[s, row + r],
            )
        return carry

    lax.fori_loop(1, 9, step, 0)
    for s in range(2):
        for h in range(2):
            n = 768 * (1 - h)
            pc[s, n : n + 256, h * 128 : h * 128 + 128] = jnp.zeros((256, 128), jnp.bfloat16)


def kernel(
    emit, tiles, ca, cb, top, bottom, left, right, c0, c1, bias, codes, fa, fb, w1, w2, *rest
):
    keyed = (None, None)
    if emit:
        oa, ob, *rest = rest
        keyed = (rest[0], rest[1])
        rest = rest[2:]
    else:
        oa, ob, *rest = rest
    kc, ke, vt, sc, pc, ct, mx, sm = rest
    centers = (ca, cb)
    feats = (fa, fb)
    outs = (oa, ob)
    across = tiles[1]
    last = tiles[0] * tiles[1] - 1
    scale = LOG2E / 128.0**0.5
    j = pl.program_id(0)

    def place(t):
        t = jnp.clip(t, 0, last)
        return t // across, t % across

    sent = jnp.asarray(SENT, jnp.bfloat16)

    def tile_of(s, ty, tx):
        raw = centers[s][pl.ds(ty * T, T), pl.ds(pl.multiple_of(tx * T, T), T), :]
        raw = raw.reshape(256, 128)
        return raw, jnp.where(raw == sent, jnp.zeros_like(raw), raw)

    def score(s, t):
        ty, tx = place(t)
        k = 1 - s
        _, query = tile_of(s, ty, tx)
        full = jnp.concatenate([query, codes[ty & 1, tx & 1]], axis=1)
        best = [None, None]
        for i in range(2):
            rows = pl.ds(2 * ty + 2 * i, 2)
            cols = pl.ds(tx, 2)
            keys = jnp.concatenate(
                [
                    kc[k, rows, cols].reshape(512, 128),
                    ke[k, rows, cols].reshape(512, 128),
                ],
                axis=1,
            )
            scores = lax.dot_general(
                keys, full, (((1,), (1,)), ((), ())), preferred_element_type=jnp.float32
            )
            for h in range(2):
                lo, hi = max(256 * h, 512 * i), min(256 * h + 768, 512 * i + 512)
                part = scores[lo - 512 * i : hi - 512 * i, h * 128 : h * 128 + 128]
                sc[s, lo:hi, h * 128 : h * 128 + 128] = part
                top_now = part.reshape((hi - lo) // 8, 8, 128).max(0)
                best[h] = top_now if best[h] is None else jnp.maximum(best[h], top_now)
            yield
        for h in range(2):
            mx[s, :, h * 128 : h * 128 + 128] = best[h]
        yield

    def weigh(s):
        for h in range(2):
            lanes = slice(h * 128, h * 128 + 128)
            best = jnp.maximum(mx[s, :, lanes].max(0, keepdims=True), 0.0)
            total = jnp.zeros((8, 128), jnp.float32)
            for n in range(256 * h, 256 * h + 768, 128):
                e = jnp.exp2((sc[s, n : n + 128, lanes] - best) * scale)
                total = total + e.reshape(16, 8, 128).sum(0)
                pc[s, n : n + 128, lanes] = e.astype(jnp.bfloat16)
                if (n - 256 * h) % 256 == 128:
                    yield
            total = total.sum(0, keepdims=True) + jnp.exp2(-best * scale)
            sm[s, :, lanes] = jnp.broadcast_to(1.0 / total, (8, 128))
        yield

    def gather(s, t, slot):
        ty, tx = place(t)
        k = 1 - s
        values = jnp.concatenate(
            [vt[k, 2 * ty + i, tx + c] for i in range(4) for c in range(2)], axis=1
        )
        carried = jnp.dot(values, pc[s], preferred_element_type=jnp.float32)
        ct[slot] = (carried * sm[s][:1]).astype(jnp.bfloat16)
        yield

    def update(s, t, slot, side):
        ty, tx = place(t)
        raw, query = tile_of(s, ty, tx)
        joined = jnp.concatenate([query, ct[slot].T], axis=1)
        x = jnp.dot(joined, w1[...], preferred_element_type=jnp.float32)
        hidden = (x * (1.0 + lax.erf(x * RSQRT2))).astype(jnp.bfloat16)
        yield
        change = jnp.dot(hidden, w2[...], preferred_element_type=jnp.float32)
        free = raw.astype(jnp.float32) > LIMIT
        cols = slice(side * T, side * T + T)
        old = feats[s][:, cols].reshape(256, 128)
        new = jnp.where(free, old, old + change)
        outs[s][:, cols] = new.reshape(T, T, 128)
        if emit:
            next_key = jnp.where(free, SENT, new).astype(jnp.bfloat16)
            keyed[s][:, cols] = next_key.reshape(T, T, 128)
        yield

    def run(begin, end):
        for u in range(4):
            s, t = u % 2, 2 * j + u // 2
            stages = []
            if not begin:
                stages.append(update(s, t - 2, u, u // 2))
            if not (begin and u == 0) and not (end and u > 0):
                stages.append(gather(1 - s, 2 * j + (u + 1) // 2 - 1, (u + 3) % 4))
            if not end:
                stages.append(score(1 - s, 2 * j + (u + 1) // 2))
                stages.append(weigh(s))
            while stages:
                stages = [stage for stage in stages if next(stage, True) is None]

    steps = (last + 1) // 2

    @pl.when(j == 0)
    def _():
        assemble(centers, top, bottom, left, right, (c0, c1), bias, kc, ke, vt, pc)
        for unused in score(0, 0):
            pass
        run(True, False)

    @pl.when((j > 0) & (j < steps))
    def _():
        run(False, False)

    @pl.when(j == steps)
    def _():
        run(False, True)


def one_pass(emit, centers, rims, marks, feat_a, feat_b, first_weight, second_weight):
    rows, cols, channels = feat_a.shape
    tiles = (rows // T, cols // T)
    count = tiles[0] * tiles[1]
    whole = pl.BlockSpec(memory_space=pltpu.VMEM)

    def at(j):
        t = jnp.clip(2 * (j - 1), 0, count - 2)
        return t // tiles[1], (t % tiles[1]) // 2, 0

    tile = pl.BlockSpec((T, 2 * T, channels), at)
    out_shape = [jax.ShapeDtypeStruct(feat_a.shape, jnp.float32)] * 2
    out_specs = [tile, tile]
    if emit:
        out_shape += [jax.ShapeDtypeStruct(feat_a.shape, jnp.bfloat16)] * 2
        out_specs += [tile, tile]
    blocks = (2, (rows + 2 * R) // 8, (cols + 2 * R) // T, 128, 128)
    flops = 2 * 16 * (2 * 1024 * 256 * 256 * 2 + 256 * 256 * 384 * 2)
    return pl.pallas_call(
        functools.partial(kernel, emit, tiles),
        grid=(count // 2 + 1,),
        in_specs=[whole] * 10 + [tile, tile, whole, whole],
        out_specs=out_specs,
        out_shape=out_shape,
        scratch_shapes=[
            pltpu.VMEM(blocks, jnp.bfloat16),
            pltpu.VMEM(blocks, jnp.bfloat16),
            pltpu.VMEM(blocks, jnp.bfloat16),
            pltpu.VMEM((2, 1024, 256), jnp.float32),
            pltpu.VMEM((2, 1024, 256), jnp.bfloat16),
            pltpu.VMEM((4, 128, 256), jnp.bfloat16),
            pltpu.VMEM((2, 8, 256), jnp.float32),
            pltpu.VMEM((2, 8, 256), jnp.float32),
        ],
        compiler_params=pltpu.CompilerParams(
            dimension_semantics=("arbitrary",), vmem_limit_bytes=44 << 20
        ),
        cost_estimate=pl.CostEstimate(
            flops=flops, bytes_accessed=14 << 20, transcendentals=2 * 16 * 768 * 256
        ),
        name="match_pass",
    )(*centers, *rims, *marks, feat_a, feat_b, first_weight, second_weight)


def shifted(cells, axis, up):
    count = lax.axis_size(axis)
    me = lax.axis_index(axis)
    if up:
        pairs = [(i, i + 1) for i in range(count - 1)]
        edge = me == 0
    else:
        pairs = [(i + 1, i) for i in range(count - 1)]
        edge = me == count - 1
    got = lax.ppermute(cells, axis, pairs)
    return jnp.where(edge, jnp.asarray(SENT, got.dtype), got)


def exchange(centers):
    def both(rows, cols):
        return jnp.stack([center[rows, cols] for center in centers])

    near, far, all_cells = slice(0, R), slice(-R, None), slice(None)
    top = shifted(both(far, all_cells), "gy", True)
    bottom = shifted(both(near, all_cells), "gy", False)
    left = shifted(both(all_cells, far), "gx", True)
    right = shifted(both(all_cells, near), "gx", False)
    head, tail = (
        jnp.concatenate([top[:, :, side], bottom[:, :, side]], axis=1) for side in (near, far)
    )
    return top, bottom, left, right, shifted(tail, "gx", True), shifted(head, "gx", False)


def local(feat_a, feat_b, occ_a, occ_b, first_weight, second_weight):
    centers = [
        jnp.where(occ[..., None] > 0, feat, SENT).astype(jnp.bfloat16)
        for feat, occ in ((feat_a, occ_a), (feat_b, occ_b))
    ]
    marks = tables()
    weights = (first_weight, second_weight * jnp.asarray(0.5, second_weight.dtype))
    rims = exchange(centers)
    feat_a, feat_b, *centers = one_pass(True, centers, rims, marks, feat_a, feat_b, *weights)
    rims = exchange(centers)
    return tuple(one_pass(False, centers, rims, marks, feat_a, feat_b, *weights))


def solution(mesh):
    in_specs = (P("gy", "gx", None), P("gy", "gx", None), P("gy", "gx"), P("gy", "gx"), P(), P())
    out_specs = (P("gy", "gx", None), P("gy", "gx", None))
    return jax.shard_map(local, mesh=mesh, in_specs=in_specs, out_specs=out_specs, check_vma=False)
```

time: 114 us -> 109 us (0.956)
  the two profiles are of different devices: /device:TPU:57 before, /device:TPU:27 now
where the time goes in v1:
time: 109 us
  starting transfers between devices  49.6 us (46%)
  Pallas kernels  36.6 us (34%)
  waiting for transfers between devices  11.7 us (11%)
  other arithmetic  9.41 us (9%)
  between operations  1.17 us (1%)
    ppermute x12, starting transfers between devices, shifted(): got = lax.ppermute(cells, axis, pairs)  49.6 us
    pallas_call x2, Pallas kernels, one_pass(): pl.pallas_call(functools.partial(kernel, emit, tiles), grid=(count // 2 +...  36.6 us
    ppermute x12, waiting for transfers between devices, shifted(): got = lax.ppermute(cells, axis, pairs)  11.7 us
    another operation x8, other arithmetic, both(): return jnp.stack([center[rows, cols] for center in centers])  3.02 us
    convert_element_type x2, other arithmetic, local(): jnp.where(occ[..., None] > 0, feat, SENT).astype(jnp.bfloat16)  2.66 us
  transfers between devices with their start and end apart: 12, of which 4 were waited for; matrix products, arithmetic and copies ran while one was open for 4% of the time, Pallas kernels for 0%

profile of v1, /device:TPU:27, one launch (start us, length us, event | category | flops | bytes accessed | tf_op | source)
XLA Modules:
  0.0 108.7 jit_solution(5836552661141219390)
XLA Ops:
  0.6 0.9 broadcast_compare_fusion.1
  1.6 0.8 broadcast_compare_fusion
  2.3 1.9 %select_convert_fusion.cb = bf16[64,64,128]{2,1,0:T(8,128)(2,1)S(1)} fusion(f32[64,64,128]{2,1,0:T(8,128)} %fb.1, pred[64,64]{1,0:T(8,128)(4,1)S(1)} %broadcast_compare_fusion), kind=kLoop, calls=%fused_computation | loop fusion | flops 524288 | bytes 3149824 | tf_op jit(solution)/shard_map/convert_element_type | solution.py:290
  5.1 0.7 pad_maximum_fusion
  5.8 4.0 %collective-permute-start = (bf16[2,8,64,128]{3,2,1,0:T(8,128)(2,1)}, bf16[2,8,64,128]{3,2,1,0:T(8,128)(2,1)}, u32[]{:S(2)}, u32[]{:S(2)}) collective-permute-start(bf16[2,8,64,128]{3,2,1,0:T(8,128)(2,1)} %pad_maximum_fusion), channel_id=1, source_target_pairs={{0,16},{16,32},{32,48},{48,64},{64,80},{80,96},{96,112},{112,128},... | collective-permute-start | bytes 786440 | tf_op jit(solution)/shard_map/ppermute | solution.py:269
  9.8 0.7 pad_maximum_fusion.1
  10.5 1.9 %collective-permute-start.1 = (bf16[2,8,64,128]{3,2,1,0:T(8,128)(2,1)}, bf16[2,8,64,128]{3,2,1,0:T(8,128)(2,1)S(1)}, u32[]{:S(2)}, u32[]{:S(2)}) collective-permute-start(bf16[2,8,64,128]{3,2,1,0:T(8,128)(2,1)} %pad_maximum_fusion.1), channel_id=1, source_target_pairs={{16,0},{32,16},{48,32},{64,48},{80,64},{96,80},{112,96},{128,112},... | collective-permute-start | bytes 786440 | tf_op jit(solution)/shard_map/ppermute | solution.py:269
  13.2 3.5 %collective-permute-start.2 = (bf16[2,64,8,128]{3,2,1,0:T(8,128)(2,1)}, bf16[2,64,8,128]{3,2,1,0:T(8,128)(2,1)S(1)}, u32[]{:S(2)}, u32[]{:S(2)}) collective-permute-start(bf16[2,64,8,128]{3,2,1,0:T(8,128)(2,1)} %pad_maximum_fusion.2), channel_id=1, source_target_pairs={{0,1},{1,2},{2,3},{3,4},{4,5},{5,6},{6,7},{7,8},{8,9},{9,10},{10,1... | collective-permute-start | bytes 786440 | tf_op jit(solution)/shard_map/ppermute | solution.py:269
  16.8 0.7 pad_maximum_fusion.3
  17.5 6.7 %collective-permute-start.3 = (bf16[2,64,8,128]{3,2,1,0:T(8,128)(2,1)}, bf16[2,64,8,128]{3,2,1,0:T(8,128)(2,1)S(1)}, u32[]{:S(2)}, u32[]{:S(2)}) collective-permute-start(bf16[2,64,8,128]{3,2,1,0:T(8,128)(2,1)} %pad_maximum_fusion.3), channel_id=1, source_target_pairs={{1,0},{2,1},{3,2},{4,3},{5,4},{6,5},{7,6},{8,7},{9,8},{10,9},{11,1... | collective-permute-start | bytes 786440 | tf_op jit(solution)/shard_map/ppermute | solution.py:269
  25.2 1.0 broadcast_select_fusion.7.top
  26.2 1.9 %collective-permute-start.4 = (bf16[2,16,8,128]{3,2,1,0:T(8,128)(2,1)S(1)}, bf16[2,16,8,128]{3,2,1,0:T(8,128)(2,1)S(1)}, u32[]{:S(2)}, u32[]{:S(2)}) collective-permute-start(bf16[2,16,8,128]{3,2,1,0:T(8,128)(2,1)S(1)} %pad_maximum_fusion.8), channel_id=1, source_target_pairs={{0,1},{1,2},{2,3},{3,4},{4,5},{5,6},{6,7},{7,8},{8,9},{9,10},{10,1... | collective-permute-start | bytes 196616 | tf_op jit(solution)/shard_map/ppermute | solution.py:269
  28.2 5.5 %collective-permute-start.5 = (bf16[2,16,8,128]{3,2,1,0:T(8,128)(2,1)S(1)}, bf16[2,16,8,128]{3,2,1,0:T(8,128)(2,1)S(1)}, u32[]{:S(2)}, u32[]{:S(2)}) collective-permute-start(bf16[2,16,8,128]{3,2,1,0:T(8,128)(2,1)S(1)} %pad_maximum_fusion.9), channel_id=1, source_target_pairs={{1,0},{2,1},{3,2},{4,3},{5,4},{6,5},{7,6},{8,7},{9,8},{10,9},{11,1... | collective-permute-start | bytes 196616 | tf_op jit(solution)/shard_map/ppermute | solution.py:269
  34.2 0.9 collective-permute-done.5
  35.1 18.7 %match_pass.2 = (f32[64,64,128]{2,1,0:T(8,128)S(1)}, f32[64,64,128]{2,1,0:T(8,128)S(1)}, bf16[64,64,128]{2,1,0:T(8,128)(2,1)S(1)}, bf16[64,64,128]{2,1,0:T(8,128)(2,1)S(1)}) custom-call(bf16[64,64,128]{2,1,0:T(8,128)(2,1)S(1)} %select_convert_fusion.1.ca, bf16[64,64,128]{2,1,0:T(8,128)(2,1)S(1)} %select_convert_fusion.cb, ...), custom_call_target="tpu_custom_call" | custom-call | flops 10200547328 | bytes 14680064 | tf_op jit(solution)/shard_map/match_pass/pallas_call | solution.py:234
  54.0 8.0 %collective-permute-start.6 = (bf16[2,8,64,128]{3,2,1,0:T(8,128)(2,1)S(1)}, bf16[2,8,64,128]{3,2,1,0:T(8,128)(2,1)S(1)}, u32[]{:S(2)}, u32[]{:S(2)}) collective-permute-start(bf16[2,8,64,128]{3,2,1,0:T(8,128)(2,1)S(1)} %pad_maximum_fusion.4), channel_id=1, source_target_pairs={{0,16},{16,32},{32,48},{48,64},{64,80},{80,96},{96,112},{112,128},... | collective-permute-start | bytes 786440 | tf_op jit(solution)/shard_map/ppermute | solution.py:269
  62.0 1.9 %collective-permute-start.8 = (bf16[2,64,8,128]{3,2,1,0:T(8,128)(2,1)S(1)}, bf16[2,64,8,128]{3,2,1,0:T(8,128)(2,1)S(1)}, u32[]{:S(2)}, u32[]{:S(2)}) collective-permute-start(bf16[2,64,8,128]{3,2,1,0:T(8,128)(2,1)S(1)} %pad_maximum_fusion.6), channel_id=1, source_target_pairs={{0,1},{1,2},{2,3},{3,4},{4,5},{5,6},{6,7},{7,8},{8,9},{9,10},{10,1... | collective-permute-start | bytes 786440 | tf_op jit(solution)/shard_map/ppermute | solution.py:269
  64.0 6.7 %collective-permute-start.9 = (bf16[2,64,8,128]{3,2,1,0:T(8,128)(2,1)S(1)}, bf16[2,64,8,128]{3,2,1,0:T(8,128)(2,1)S(1)}, u32[]{:S(2)}, u32[]{:S(2)}) collective-permute-start(bf16[2,64,8,128]{3,2,1,0:T(8,128)(2,1)S(1)} %pad_maximum_fusion.7), channel_id=1, source_target_pairs={{1,0},{2,1},{3,2},{4,3},{5,4},{6,5},{7,6},{8,7},{9,8},{10,9},{11,1... | collective-permute-start | bytes 786440 | tf_op jit(solution)/shard_map/ppermute | solution.py:269
  70.7 1.9 %collective-permute-start.7 = (bf16[2,8,64,128]{3,2,1,0:T(8,128)(2,1)S(1)}, bf16[2,8,64,128]{3,2,1,0:T(8,128)(2,1)S(1)}, u32[]{:S(2)}, u32[]{:S(2)}) collective-permute-start(bf16[2,8,64,128]{3,2,1,0:T(8,128)(2,1)S(1)} %pad_maximum_fusion.5), channel_id=1, source_target_pairs={{16,0},{32,16},{48,32},{64,48},{80,64},{96,80},{112,96},{128,112},... | collective-permute-start | bytes 786440 | tf_op jit(solution)/shard_map/ppermute | solution.py:269
  72.7 9.3 %collective-permute-done.7 = bf16[2,8,64,128]{3,2,1,0:T(8,128)(2,1)S(1)} collective-permute-done((bf16[2,8,64,128]{3,2,1,0:T(8,128)(2,1)S(1)}, bf16[2,8,64,128]{3,2,1,0:T(8,128)(2,1)S(1)}, u32[]{:S(2)}, u32[]{:S(2)}) %collective-permute-start.7) | collective-permute-done | bytes 262176 | tf_op jit(solution)/shard_map/ppermute | solution.py:269
  82.1 1.9 %collective-permute-start.10 = (bf16[2,16,8,128]{3,2,1,0:T(8,128)(2,1)S(1)}, bf16[2,16,8,128]{3,2,1,0:T(8,128)(2,1)S(1)}, u32[]{:S(2)}, u32[]{:S(2)}) collective-permute-start(bf16[2,16,8,128]{3,2,1,0:T(8,128)(2,1)S(1)} %pad_maximum_fusion.10), channel_id=1, source_target_pairs={{0,1},{1,2},{2,3},{3,4},{4,5},{5,6},{6,7},{7,8},{8,9},{9,10},{10,1... | collective-permute-start | bytes 196616 | tf_op jit(solution)/shard_map/ppermute | solution.py:269
  84.0 5.7 %collective-permute-start.11 = (bf16[2,16,8,128]{3,2,1,0:T(8,128)(2,1)S(1)}, bf16[2,16,8,128]{3,2,1,0:T(8,128)(2,1)S(1)}, u32[]{:S(2)}, u32[]{:S(2)}) collective-permute-start(bf16[2,16,8,128]{3,2,1,0:T(8,128)(2,1)S(1)} %pad_maximum_fusion.11), channel_id=1, source_target_pairs={{1,0},{2,1},{3,2},{4,3},{5,4},{6,5},{7,6},{8,7},{9,8},{10,9},{11,1... | collective-permute-start | bytes 196616 | tf_op jit(solution)/shard_map/ppermute | solution.py:269
  89.8 1.0 collective-permute-done.11
  90.8 17.9 %match_pass.3 = (f32[64,64,128]{2,1,0:T(8,128)}, f32[64,64,128]{2,1,0:T(8,128)}) custom-call(bf16[64,64,128]{2,1,0:T(8,128)(2,1)S(1)} %get-tuple-element.6.ca, bf16[64,64,128]{2,1,0:T(8,128)(2,1)S(1)} %get-tuple-element.7.cb, bf16[2,8,64,128]{3,2,1,0:T(8,128)(2,1)S(1)} %broadcast_select_fusion.6.top, ...), custom_call_target="tpu_custom_call" | custom-call | flops 10200547328 | bytes 14680064 | tf_op jit(solution)/shard_map/match_pass/pallas_call | solution.py:234
  (61 shorter events, 3.4 us)
Async XLA Ops:
  0.6 3.6 %copy-start.1 = (f32[64,64,128]{2,1,0:T(8,128)S(1)}, f32[64,64,128]{2,1,0:T(8,128)}, u32[]{:S(2)}) copy-start(f32[64,64,128]{2,1,0:T(8,128)} %fa.1) | copy-start | bytes 6291460
  5.0 19.3 %copy-start.2 = (bf16[256,128]{1,0:T(8,128)(2,1)S(1)}, bf16[256,128]{1,0:T(8,128)(2,1)}, u32[]{:S(2)}) copy-start(bf16[256,128]{1,0:T(8,128)(2,1)} %param.11) | copy-start | bytes 196612
  5.8 19.4 %collective-permute-start = (bf16[2,8,64,128]{3,2,1,0:T(8,128)(2,1)}, bf16[2,8,64,128]{3,2,1,0:T(8,128)(2,1)}, u32[]{:S(2)}, u32[]{:S(2)}) collective-permute-start(bf16[2,8,64,128]{3,2,1,0:T(8,128)(2,1)} %pad_maximum_fusion), channel_id=1, source_target_pairs={{0,16},{16,32},{32,48},{48,64},{64,80},{80,96},{96,112},{112,128},... | collective-permute-start | bytes 786440 | tf_op jit(solution)/shard_map/ppermute | solution.py:269
  10.5 15.7 %collective-permute-start.1 = (bf16[2,8,64,128]{3,2,1,0:T(8,128)(2,1)}, bf16[2,8,64,128]{3,2,1,0:T(8,128)(2,1)S(1)}, u32[]{:S(2)}, u32[]{:S(2)}) collective-permute-start(bf16[2,8,64,128]{3,2,1,0:T(8,128)(2,1)} %pad_maximum_fusion.1), channel_id=1, source_target_pairs={{16,0},{32,16},{48,32},{64,48},{80,64},{96,80},{112,96},{128,112},... | collective-permute-start | bytes 786440 | tf_op jit(solution)/shard_map/ppermute | solution.py:269
  13.2 20.5 %collective-permute-start.2 = (bf16[2,64,8,128]{3,2,1,0:T(8,128)(2,1)}, bf16[2,64,8,128]{3,2,1,0:T(8,128)(2,1)S(1)}, u32[]{:S(2)}, u32[]{:S(2)}) collective-permute-start(bf16[2,64,8,128]{3,2,1,0:T(8,128)(2,1)} %pad_maximum_fusion.2), channel_id=1, source_target_pairs={{0,1},{1,2},{2,3},{3,4},{4,5},{5,6},{6,7},{7,8},{8,9},{9,10},{10,1... | collective-permute-start | bytes 786440 | tf_op jit(solution)/shard_map/ppermute | solution.py:269
  16.8 18.3 %copy-start = (bf16[256,256]{1,0:T(8,128)(2,1)S(1)}, bf16[256,256]{1,0:T(8,128)(2,1)}, u32[]{:S(2)}) copy-start(bf16[256,256]{1,0:T(8,128)(2,1)} %w1.3) | copy-start | bytes 393220
  17.5 16.2 %collective-permute-start.3 = (bf16[2,64,8,128]{3,2,1,0:T(8,128)(2,1)}, bf16[2,64,8,128]{3,2,1,0:T(8,128)(2,1)S(1)}, u32[]{:S(2)}, u32[]{:S(2)}) collective-permute-start(bf16[2,64,8,128]{3,2,1,0:T(8,128)(2,1)} %pad_maximum_fusion.3), channel_id=1, source_target_pairs={{1,0},{2,1},{3,2},{4,3},{5,4},{6,5},{7,6},{8,7},{9,8},{10,9},{11,1... | collective-permute-start | bytes 786440 | tf_op jit(solution)/shard_map/ppermute | solution.py:269
  26.2 7.9 %collective-permute-start.4 = (bf16[2,16,8,128]{3,2,1,0:T(8,128)(2,1)S(1)}, bf16[2,16,8,128]{3,2,1,0:T(8,128)(2,1)S(1)}, u32[]{:S(2)}, u32[]{:S(2)}) collective-permute-start(bf16[2,16,8,128]{3,2,1,0:T(8,128)(2,1)S(1)} %pad_maximum_fusion.8), channel_id=1, source_target_pairs={{0,1},{1,2},{2,3},{3,4},{4,5},{5,6},{6,7},{7,8},{8,9},{9,10},{10,1... | collective-permute-start | bytes 196616 | tf_op jit(solution)/shard_map/ppermute | solution.py:269
  28.2 6.9 %collective-permute-start.5 = (bf16[2,16,8,128]{3,2,1,0:T(8,128)(2,1)S(1)}, bf16[2,16,8,128]{3,2,1,0:T(8,128)(2,1)S(1)}, u32[]{:S(2)}, u32[]{:S(2)}) collective-permute-start(bf16[2,16,8,128]{3,2,1,0:T(8,128)(2,1)S(1)} %pad_maximum_fusion.9), channel_id=1, source_target_pairs={{1,0},{2,1},{3,2},{4,3},{5,4},{6,5},{7,6},{8,7},{9,8},{10,9},{11,1... | collective-permute-start | bytes 196616 | tf_op jit(solution)/shard_map/ppermute | solution.py:269
  54.0 18.6 %collective-permute-start.6 = (bf16[2,8,64,128]{3,2,1,0:T(8,128)(2,1)S(1)}, bf16[2,8,64,128]{3,2,1,0:T(8,128)(2,1)S(1)}, u32[]{:S(2)}, u32[]{:S(2)}) collective-permute-start(bf16[2,8,64,128]{3,2,1,0:T(8,128)(2,1)S(1)} %pad_maximum_fusion.4), channel_id=1, source_target_pairs={{0,16},{16,32},{32,48},{48,64},{64,80},{80,96},{96,112},{112,128},... | collective-permute-start | bytes 786440 | tf_op jit(solution)/shard_map/ppermute | solution.py:269
  62.0 27.7 %collective-permute-start.8 = (bf16[2,64,8,128]{3,2,1,0:T(8,128)(2,1)S(1)}, bf16[2,64,8,128]{3,2,1,0:T(8,128)(2,1)S(1)}, u32[]{:S(2)}, u32[]{:S(2)}) collective-permute-start(bf16[2,64,8,128]{3,2,1,0:T(8,128)(2,1)S(1)} %pad_maximum_fusion.6), channel_id=1, source_target_pairs={{0,1},{1,2},{2,3},{3,4},{4,5},{5,6},{6,7},{7,8},{8,9},{9,10},{10,1... | collective-permute-start | bytes 786440 | tf_op jit(solution)/shard_map/ppermute | solution.py:269
  64.0 25.8 %collective-permute-start.9 = (bf16[2,64,8,128]{3,2,1,0:T(8,128)(2,1)S(1)}, bf16[2,64,8,128]{3,2,1,0:T(8,128)(2,1)S(1)}, u32[]{:S(2)}, u32[]{:S(2)}) collective-permute-start(bf16[2,64,8,128]{3,2,1,0:T(8,128)(2,1)S(1)} %pad_maximum_fusion.7), channel_id=1, source_target_pairs={{1,0},{2,1},{3,2},{4,3},{5,4},{6,5},{7,6},{8,7},{9,8},{10,9},{11,1... | collective-permute-start | bytes 786440 | tf_op jit(solution)/shard_map/ppermute | solution.py:269
  70.7 11.3 %collective-permute-start.7 = (bf16[2,8,64,128]{3,2,1,0:T(8,128)(2,1)S(1)}, bf16[2,8,64,128]{3,2,1,0:T(8,128)(2,1)S(1)}, u32[]{:S(2)}, u32[]{:S(2)}) collective-permute-start(bf16[2,8,64,128]{3,2,1,0:T(8,128)(2,1)S(1)} %pad_maximum_fusion.5), channel_id=1, source_target_pairs={{16,0},{32,16},{48,32},{64,48},{80,64},{96,80},{112,96},{128,112},... | collective-permute-start | bytes 786440 | tf_op jit(solution)/shard_map/ppermute | solution.py:269
  82.1 7.7 %collective-permute-start.10 = (bf16[2,16,8,128]{3,2,1,0:T(8,128)(2,1)S(1)}, bf16[2,16,8,128]{3,2,1,0:T(8,128)(2,1)S(1)}, u32[]{:S(2)}, u32[]{:S(2)}) collective-permute-start(bf16[2,16,8,128]{3,2,1,0:T(8,128)(2,1)S(1)} %pad_maximum_fusion.10), channel_id=1, source_target_pairs={{0,1},{1,2},{2,3},{3,4},{4,5},{5,6},{6,7},{7,8},{8,9},{9,10},{10,1... | collective-permute-start | bytes 196616 | tf_op jit(solution)/shard_map/ppermute | solution.py:269
  84.0 6.8 %collective-permute-start.11 = (bf16[2,16,8,128]{3,2,1,0:T(8,128)(2,1)S(1)}, bf16[2,16,8,128]{3,2,1,0:T(8,128)(2,1)S(1)}, u32[]{:S(2)}, u32[]{:S(2)}) collective-permute-start(bf16[2,16,8,128]{3,2,1,0:T(8,128)(2,1)S(1)} %pad_maximum_fusion.11), channel_id=1, source_target_pairs={{1,0},{2,1},{3,2},{4,3},{5,4},{6,5},{7,6},{8,7},{9,8},{10,9},{11,1... | collective-permute-start | bytes 196616 | tf_op jit(solution)/shard_map/ppermute | solution.py:269

commit v2 on v1

--- a/solution.py
+++ b/solution.py
@@ -34,13 +34,10 @@
     return bias, jnp.where(hit, 1.0, 0.0).astype(jnp.bfloat16)
 
 
-def assemble(centers, top, bottom, left, right, corners, bias, kc, ke, vt, pc):
+def assemble(centers, top, bottom, left, right, bias, kc, ke, vt, pc):
     sent = jnp.asarray(SENT, jnp.bfloat16)
 
-    def group(s, rg, row_of, left_of, right_of):
-        lines = [
-            jnp.concatenate([left_of(r), row_of(r), right_of(r)], axis=0) for r in range(8)
-        ]
+    def group(s, rg, lines):
         for cg in range(5):
             raw = jnp.concatenate([line[cg * T : (cg + 1) * T] for line in lines], axis=0)
             free = raw == sent
@@ -50,25 +47,19 @@
             ke[s, rg, cg] = jnp.where(free, jnp.full_like(raw, -BIG), bias[rg & 3, cg & 1])
 
     for s in range(2):
-        for rg, source, first in ((0, top, 0), (9, bottom, R)):
-            group(
-                s,
-                rg,
-                lambda r: source[s, r],
-                lambda r: corners[0][s, first + r],
-                lambda r: corners[1][s, first + r],
-            )
+        for rg, source in ((0, top), (9, bottom)):
+            group(s, rg, [source[s, r] for r in range(8)])
 
     def step(rg, carry):
         row = (rg - 1) * 8
         for s in range(2):
-            group(
-                s,
-                rg,
-                lambda r: centers[s][row + r],
-                lambda r: left[s, row + r],
-                lambda r: right[s, row + r],
-            )
+            lines = [
+                jnp.concatenate(
+                    [left[s, row + r], centers[s][row + r], right[s, row + r]], axis=0
+                )
+                for r in range(8)
+            ]
+            group(s, rg, lines)
         return carry
 
     lax.fori_loop(1, 9, step, 0)
@@ -79,7 +70,7 @@
 
 
 def kernel(
-    emit, tiles, ca, cb, top, bottom, left, right, c0, c1, bias, codes, fa, fb, w1, w2, *rest
+    emit, tiles, ca, cb, top, bottom, left, right, bias, codes, fa, fb, w1, w2, *rest
 ):
     keyed = (None, None)
     if emit:
@@ -199,7 +190,7 @@
 
     @pl.when(j == 0)
     def _():
-        assemble(centers, top, bottom, left, right, (c0, c1), bias, kc, ke, vt, pc)
+        assemble(centers, top, bottom, left, right, bias, kc, ke, vt, pc)
         for unused in score(0, 0):
             pass
         run(True, False)
@@ -234,7 +225,7 @@
     return pl.pallas_call(
         functools.partial(kernel, emit, tiles),
         grid=(count // 2 + 1,),
-        in_specs=[whole] * 10 + [tile, tile, whole, whole],
+        in_specs=[whole] * 8 + [tile, tile, whole, whole],
         out_specs=out_specs,
         out_shape=out_shape,
         scratch_shapes=[
@@ -275,14 +266,21 @@
         return jnp.stack([center[rows, cols] for center in centers])
 
     near, far, all_cells = slice(0, R), slice(-R, None), slice(None)
-    top = shifted(both(far, all_cells), "gy", True)
-    bottom = shifted(both(near, all_cells), "gy", False)
+
+    def ends(cols):
+        return jnp.concatenate([both(near, cols), both(far, cols)], axis=1)
+
+    west = shifted(ends(far), "gx", True)
+    east = shifted(ends(near), "gx", False)
     left = shifted(both(all_cells, far), "gx", True)
     right = shifted(both(all_cells, near), "gx", False)
-    head, tail = (
-        jnp.concatenate([top[:, :, side], bottom[:, :, side]], axis=1) for side in (near, far)
-    )
-    return top, bottom, left, right, shifted(tail, "gx", True), shifted(head, "gx", False)
+
+    def wide(rows):
+        return jnp.concatenate([west[:, rows], both(rows, all_cells), east[:, rows]], axis=2)
+
+    top = shifted(wide(far), "gy", True)
+    bottom = shifted(wide(near), "gy", False)
+    return top, bottom, left, right
 
 
 def local(feat_a, feat_b, occ_a, occ_b, first_weight, second_weight):

time: 109 us -> 109 us (level)
  starting transfers between devices: 49.6 us -> 41.8 us
  waiting for transfers between devices: 11.7 us -> 18.4 us
    ppermute x12, starting transfers between devices: 49.6 us -> 41.8 us  [shifted(): got = lax.ppermute(cells, axis, pairs)]
    ppermute x12, waiting for transfers between devices: 11.7 us -> 18.4 us  [shifted(): got = lax.ppermute(cells, axis, pairs)]
    select_n x12, other arithmetic: 1.21 us -> 2.96 us  [shifted(): return jnp.where(edge, jnp.asarray(SENT, got.dtype), got)]
    another operation x8 -> x4, other arithmetic: 3.02 us -> 1.51 us  [both(): return jnp.stack([center[rows, cols] for center in centers])]
  transfers between devices with their start and end apart: 12 -> 12, of which waited for: 4 -> 4; matrix products, arithmetic and copies ran while one was open for 4% -> 6% of each run, Pallas kernels for 0% -> 0%
where the time goes in v2:
time: 109 us
  starting transfers between devices  41.8 us (38%)
  Pallas kernels  36.6 us (34%)
  waiting for transfers between devices  18.4 us (17%)
  other arithmetic  10.4 us (10%)
  between operations  1.18 us (1%)
    ppermute x12, starting transfers between devices, shifted(): got = lax.ppermute(cells, axis, pairs)  41.8 us
    pallas_call x2, Pallas kernels, one_pass(): pl.pallas_call(functools.partial(kernel, emit, tiles), grid=(count // 2 +...  36.6 us
    ppermute x12, waiting for transfers between devices, shifted(): got = lax.ppermute(cells, axis, pairs)  18.4 us
    select_n x12, other arithmetic, shifted(): return jnp.where(edge, jnp.asarray(SENT, got.dtype), got)  2.96 us
    convert_element_type x2, other arithmetic, local(): jnp.where(occ[..., None] > 0, feat, SENT).astype(jnp.bfloat16)  2.66 us
  transfers between devices with their start and end apart: 12, of which 4 were waited for; matrix products, arithmetic and copies ran while one was open for 6% of the time, Pallas kernels for 0%

profile of v2, /device:TPU:27, one launch (start us, length us, event | category | flops | bytes accessed | tf_op | source)
XLA Modules:
  0.0 108.7 jit_solution(3612649650756081838)
XLA Ops:
  0.6 0.9 broadcast_compare_fusion.1
  1.6 0.8 broadcast_compare_fusion
  2.3 1.9 %select_convert_fusion.cb = bf16[64,64,128]{2,1,0:T(8,128)(2,1)S(1)} fusion(f32[64,64,128]{2,1,0:T(8,128)} %fb.1, pred[64,64]{1,0:T(8,128)(4,1)S(1)} %broadcast_compare_fusion), kind=kLoop, calls=%fused_computation | loop fusion | flops 524288 | bytes 3149824 | tf_op jit(solution)/shard_map/convert_element_type | solution.py:288
  5.1 7.5 %collective-permute-start.1 = (bf16[2,16,8,128]{3,2,1,0:T(8,128)(2,1)S(1)}, bf16[2,16,8,128]{3,2,1,0:T(8,128)(2,1)}, u32[]{:S(2)}, u32[]{:S(2)}) collective-permute-start(bf16[2,16,8,128]{3,2,1,0:T(8,128)(2,1)S(1)} %maximum_maximum_fusion.1), channel_id=1, source_target_pairs={{1,0},{2,1},{3,2},{4,3},{5,4},{6,5},{7,6},{8,7},{9,8},{10,9},{11,1... | collective-permute-start | bytes 196616 | tf_op jit(solution)/shard_map/ppermute | solution.py:260
  13.2 1.9 %collective-permute-start = (bf16[2,16,8,128]{3,2,1,0:T(8,128)(2,1)}, bf16[2,16,8,128]{3,2,1,0:T(8,128)(2,1)}, u32[]{:S(2)}, u32[]{:S(2)}) collective-permute-start(bf16[2,16,8,128]{3,2,1,0:T(8,128)(2,1)} %maximum_maximum_fusion), channel_id=1, source_target_pairs={{0,1},{1,2},{2,3},{3,4},{4,5},{5,6},{6,7},{7,8},{8,9},{9,10},{10,1... | collective-permute-start | bytes 196616 | tf_op jit(solution)/shard_map/ppermute | solution.py:260
  15.9 1.9 %collective-permute-start.4 = (bf16[2,64,8,128]{3,2,1,0:T(8,128)(2,1)}, bf16[2,64,8,128]{3,2,1,0:T(8,128)(2,1)S(1)}, u32[]{:S(2)}, u32[]{:S(2)}) collective-permute-start(bf16[2,64,8,128]{3,2,1,0:T(8,128)(2,1)} %pad_maximum_fusion.4), channel_id=1, source_target_pairs={{0,1},{1,2},{2,3},{3,4},{4,5},{5,6},{6,7},{7,8},{8,9},{9,10},{10,1... | collective-permute-start | bytes 786440 | tf_op jit(solution)/shard_map/ppermute | solution.py:260
  18.6 5.5 %collective-permute-start.5 = (bf16[2,64,8,128]{3,2,1,0:T(8,128)(2,1)}, bf16[2,64,8,128]{3,2,1,0:T(8,128)(2,1)}, u32[]{:S(2)}, u32[]{:S(2)}) collective-permute-start(bf16[2,64,8,128]{3,2,1,0:T(8,128)(2,1)} %pad_maximum_fusion.5), channel_id=1, source_target_pairs={{1,0},{2,1},{3,2},{4,3},{5,4},{6,5},{7,6},{8,7},{9,8},{10,9},{11,1... | collective-permute-start | bytes 786440 | tf_op jit(solution)/shard_map/ppermute | solution.py:260
  25.0 0.9 broadcast_select_fusion.9
  25.9 0.9 broadcast_select_fusion.11
  26.8 5.1 %collective-permute-start.2 = (bf16[2,8,80,128]{3,2,1,0:T(8,128)(2,1)S(1)}, bf16[2,8,80,128]{3,2,1,0:T(8,128)(2,1)S(1)}, u32[]{:S(2)}, u32[]{:S(2)}) collective-permute-start(bf16[2,8,80,128]{3,2,1,0:T(8,128)(2,1)S(1)} %pad_maximum_fusion), channel_id=1, source_target_pairs={{0,16},{16,32},{32,48},{48,64},{64,80},{80,96},{96,112},{112,128},... | collective-permute-start | bytes 983048 | tf_op jit(solution)/shard_map/ppermute | solution.py:260
  32.0 1.9 %collective-permute-start.3 = (bf16[2,8,80,128]{3,2,1,0:T(8,128)(2,1)S(1)}, bf16[2,8,80,128]{3,2,1,0:T(8,128)(2,1)S(1)}, u32[]{:S(2)}, u32[]{:S(2)}) collective-permute-start(bf16[2,8,80,128]{3,2,1,0:T(8,128)(2,1)S(1)} %pad_maximum_fusion.1), channel_id=1, source_target_pairs={{16,0},{32,16},{48,32},{64,48},{80,64},{96,80},{112,96},{128,112},... | collective-permute-start | bytes 983048 | tf_op jit(solution)/shard_map/ppermute | solution.py:260
  33.9 1.0 broadcast_select_fusion.5.right
  34.9 1.0 collective-permute-done.2
  36.0 8.0 %collective-permute-done.3 = bf16[2,8,80,128]{3,2,1,0:T(8,128)(2,1)S(1)} collective-permute-done((bf16[2,8,80,128]{3,2,1,0:T(8,128)(2,1)S(1)}, bf16[2,8,80,128]{3,2,1,0:T(8,128)(2,1)S(1)}, u32[]{:S(2)}, u32[]{:S(2)}) %collective-permute-start.3) | collective-permute-done | bytes 327712 | tf_op jit(solution)/shard_map/ppermute | solution.py:260
  44.0 18.7 %match_pass.2 = (f32[64,64,128]{2,1,0:T(8,128)S(1)}, f32[64,64,128]{2,1,0:T(8,128)S(1)}, bf16[64,64,128]{2,1,0:T(8,128)(2,1)S(1)}, bf16[64,64,128]{2,1,0:T(8,128)(2,1)S(1)}) custom-call(bf16[64,64,128]{2,1,0:T(8,128)(2,1)S(1)} %select_convert_fusion.1.ca, bf16[64,64,128]{2,1,0:T(8,128)(2,1)S(1)} %select_convert_fusion.cb, ...), custom_call_target="tpu_custom_call" | custom-call | flops 10200547328 | bytes 14680064 | tf_op jit(solution)/shard_map/match_pass/pallas_call | solution.py:225
  62.9 4.2 %collective-permute-start.7 = (bf16[2,16,8,128]{3,2,1,0:T(8,128)(2,1)S(1)}, bf16[2,16,8,128]{3,2,1,0:T(8,128)(2,1)S(1)}, u32[]{:S(2)}, u32[]{:S(2)}) collective-permute-start(bf16[2,16,8,128]{3,2,1,0:T(8,128)(2,1)S(1)} %maximum_maximum_fusion.3), channel_id=1, source_target_pairs={{1,0},{2,1},{3,2},{4,3},{5,4},{6,5},{7,6},{8,7},{9,8},{10,9},{11,1... | collective-permute-start | bytes 196616 | tf_op jit(solution)/shard_map/ppermute | solution.py:260
  67.2 1.9 %collective-permute-start.6 = (bf16[2,16,8,128]{3,2,1,0:T(8,128)(2,1)S(1)}, bf16[2,16,8,128]{3,2,1,0:T(8,128)(2,1)S(1)}, u32[]{:S(2)}, u32[]{:S(2)}) collective-permute-start(bf16[2,16,8,128]{3,2,1,0:T(8,128)(2,1)S(1)} %maximum_maximum_fusion.2), channel_id=1, source_target_pairs={{0,1},{1,2},{2,3},{3,4},{4,5},{5,6},{6,7},{7,8},{8,9},{9,10},{10,1... | collective-permute-start | bytes 196616 | tf_op jit(solution)/shard_map/ppermute | solution.py:260
  69.2 1.9 %collective-permute-start.10 = (bf16[2,64,8,128]{3,2,1,0:T(8,128)(2,1)S(1)}, bf16[2,64,8,128]{3,2,1,0:T(8,128)(2,1)S(1)}, u32[]{:S(2)}, u32[]{:S(2)}) collective-permute-start(bf16[2,64,8,128]{3,2,1,0:T(8,128)(2,1)S(1)} %pad_maximum_fusion.6), channel_id=1, source_target_pairs={{0,1},{1,2},{2,3},{3,4},{4,5},{5,6},{6,7},{7,8},{8,9},{9,10},{10,1... | collective-permute-start | bytes 786440 | tf_op jit(solution)/shard_map/ppermute | solution.py:260
  71.1 5.5 %collective-permute-start.11 = (bf16[2,64,8,128]{3,2,1,0:T(8,128)(2,1)S(1)}, bf16[2,64,8,128]{3,2,1,0:T(8,128)(2,1)S(1)}, u32[]{:S(2)}, u32[]{:S(2)}) collective-permute-start(bf16[2,64,8,128]{3,2,1,0:T(8,128)(2,1)S(1)} %pad_maximum_fusion.7), channel_id=1, source_target_pairs={{1,0},{2,1},{3,2},{4,3},{5,4},{6,5},{7,6},{8,7},{9,8},{10,9},{11,1... | collective-permute-start | bytes 786440 | tf_op jit(solution)/shard_map/ppermute | solution.py:260
  76.7 2.0 %collective-permute-start.8 = (bf16[2,8,80,128]{3,2,1,0:T(8,128)(2,1)S(1)}, bf16[2,8,80,128]{3,2,1,0:T(8,128)(2,1)S(1)}, u32[]{:S(2)}, u32[]{:S(2)}) collective-permute-start(bf16[2,8,80,128]{3,2,1,0:T(8,128)(2,1)S(1)} %pad_maximum_fusion.2), channel_id=1, source_target_pairs={{0,16},{16,32},{32,48},{48,64},{64,80},{80,96},{96,112},{112,128},... | collective-permute-start | bytes 983048 | tf_op jit(solution)/shard_map/ppermute | solution.py:260
  78.8 2.5 %collective-permute-start.9 = (bf16[2,8,80,128]{3,2,1,0:T(8,128)(2,1)S(1)}, bf16[2,8,80,128]{3,2,1,0:T(8,128)(2,1)S(1)}, u32[]{:S(2)}, u32[]{:S(2)}) collective-permute-start(bf16[2,8,80,128]{3,2,1,0:T(8,128)(2,1)S(1)} %pad_maximum_fusion.3), channel_id=1, source_target_pairs={{16,0},{32,16},{48,32},{64,48},{80,64},{96,80},{112,96},{128,112},... | collective-permute-start | bytes 983048 | tf_op jit(solution)/shard_map/ppermute | solution.py:260
  81.4 1.3 %collective-permute-done.8 = bf16[2,8,80,128]{3,2,1,0:T(8,128)(2,1)S(1)} collective-permute-done((bf16[2,8,80,128]{3,2,1,0:T(8,128)(2,1)S(1)}, bf16[2,8,80,128]{3,2,1,0:T(8,128)(2,1)S(1)}, u32[]{:S(2)}, u32[]{:S(2)}) %collective-permute-start.8) | collective-permute-done | bytes 327712 | tf_op jit(solution)/shard_map/ppermute | solution.py:260
  82.8 8.0 %collective-permute-done.9 = bf16[2,8,80,128]{3,2,1,0:T(8,128)(2,1)S(1)} collective-permute-done((bf16[2,8,80,128]{3,2,1,0:T(8,128)(2,1)S(1)}, bf16[2,8,80,128]{3,2,1,0:T(8,128)(2,1)S(1)}, u32[]{:S(2)}, u32[]{:S(2)}) %collective-permute-start.9) | collective-permute-done | bytes 327712 | tf_op jit(solution)/shard_map/ppermute | solution.py:260
  90.8 17.9 %match_pass.3 = (f32[64,64,128]{2,1,0:T(8,128)}, f32[64,64,128]{2,1,0:T(8,128)}) custom-call(bf16[64,64,128]{2,1,0:T(8,128)(2,1)S(1)} %get-tuple-element.6.ca, bf16[64,64,128]{2,1,0:T(8,128)(2,1)S(1)} %get-tuple-element.7.cb, bf16[2,8,80,128]{3,2,1,0:T(8,128)(2,1)S(1)} %broadcast_select_fusion.2.top, ...), custom_call_target="tpu_custom_call" | custom-call | flops 10200547328 | bytes 14680064 | tf_op jit(solution)/shard_map/match_pass/pallas_call | solution.py:225
  (64 shorter events, 4.4 us)
Async XLA Ops:
  0.6 3.6 %copy-start.1 = (f32[64,64,128]{2,1,0:T(8,128)S(1)}, f32[64,64,128]{2,1,0:T(8,128)}, u32[]{:S(2)}) copy-start(f32[64,64,128]{2,1,0:T(8,128)} %fa.1) | copy-start | bytes 6291460
  5.0 19.9 %copy-start.2 = (bf16[256,128]{1,0:T(8,128)(2,1)S(1)}, bf16[256,128]{1,0:T(8,128)(2,1)}, u32[]{:S(2)}) copy-start(bf16[256,128]{1,0:T(8,128)(2,1)} %param.11) | copy-start | bytes 196612
  5.1 19.9 %collective-permute-start.1 = (bf16[2,16,8,128]{3,2,1,0:T(8,128)(2,1)S(1)}, bf16[2,16,8,128]{3,2,1,0:T(8,128)(2,1)}, u32[]{:S(2)}, u32[]{:S(2)}) collective-permute-start(bf16[2,16,8,128]{3,2,1,0:T(8,128)(2,1)S(1)} %maximum_maximum_fusion.1), channel_id=1, source_target_pairs={{1,0},{2,1},{3,2},{4,3},{5,4},{6,5},{7,6},{8,7},{9,8},{10,9},{11,1... | collective-permute-start | bytes 196616 | tf_op jit(solution)/shard_map/ppermute | solution.py:260
  13.2 12.7 %collective-permute-start = (bf16[2,16,8,128]{3,2,1,0:T(8,128)(2,1)}, bf16[2,16,8,128]{3,2,1,0:T(8,128)(2,1)}, u32[]{:S(2)}, u32[]{:S(2)}) collective-permute-start(bf16[2,16,8,128]{3,2,1,0:T(8,128)(2,1)} %maximum_maximum_fusion), channel_id=1, source_target_pairs={{0,1},{1,2},{2,3},{3,4},{4,5},{5,6},{6,7},{7,8},{8,9},{9,10},{10,1... | collective-permute-start | bytes 196616 | tf_op jit(solution)/shard_map/ppermute | solution.py:260
  15.9 18.0 %collective-permute-start.4 = (bf16[2,64,8,128]{3,2,1,0:T(8,128)(2,1)}, bf16[2,64,8,128]{3,2,1,0:T(8,128)(2,1)S(1)}, u32[]{:S(2)}, u32[]{:S(2)}) collective-permute-start(bf16[2,64,8,128]{3,2,1,0:T(8,128)(2,1)} %pad_maximum_fusion.4), channel_id=1, source_target_pairs={{0,1},{1,2},{2,3},{3,4},{4,5},{5,6},{6,7},{7,8},{8,9},{9,10},{10,1... | collective-permute-start | bytes 786440 | tf_op jit(solution)/shard_map/ppermute | solution.py:260
  18.6 15.4 %collective-permute-start.5 = (bf16[2,64,8,128]{3,2,1,0:T(8,128)(2,1)}, bf16[2,64,8,128]{3,2,1,0:T(8,128)(2,1)}, u32[]{:S(2)}, u32[]{:S(2)}) collective-permute-start(bf16[2,64,8,128]{3,2,1,0:T(8,128)(2,1)} %pad_maximum_fusion.5), channel_id=1, source_target_pairs={{1,0},{2,1},{3,2},{4,3},{5,4},{6,5},{7,6},{8,7},{9,8},{10,9},{11,1... | collective-permute-start | bytes 786440 | tf_op jit(solution)/shard_map/ppermute | solution.py:260
  25.0 19.0 %copy-start = (bf16[256,256]{1,0:T(8,128)(2,1)S(1)}, bf16[256,256]{1,0:T(8,128)(2,1)}, u32[]{:S(2)}) copy-start(bf16[256,256]{1,0:T(8,128)(2,1)} %w1.3) | copy-start | bytes 393220
  26.8 9.1 %collective-permute-start.2 = (bf16[2,8,80,128]{3,2,1,0:T(8,128)(2,1)S(1)}, bf16[2,8,80,128]{3,2,1,0:T(8,128)(2,1)S(1)}, u32[]{:S(2)}, u32[]{:S(2)}) collective-permute-start(bf16[2,8,80,128]{3,2,1,0:T(8,128)(2,1)S(1)} %pad_maximum_fusion), channel_id=1, source_target_pairs={{0,16},{16,32},{32,48},{48,64},{64,80},{80,96},{96,112},{112,128},... | collective-permute-start | bytes 983048 | tf_op jit(solution)/shard_map/ppermute | solution.py:260
  32.0 12.0 %collective-permute-start.3 = (bf16[2,8,80,128]{3,2,1,0:T(8,128)(2,1)S(1)}, bf16[2,8,80,128]{3,2,1,0:T(8,128)(2,1)S(1)}, u32[]{:S(2)}, u32[]{:S(2)}) collective-permute-start(bf16[2,8,80,128]{3,2,1,0:T(8,128)(2,1)S(1)} %pad_maximum_fusion.1), channel_id=1, source_target_pairs={{16,0},{32,16},{48,32},{64,48},{80,64},{96,80},{112,96},{128,112},... | collective-permute-start | bytes 983048 | tf_op jit(solution)/shard_map/ppermute | solution.py:260
  62.9 13.7 %collective-permute-start.7 = (bf16[2,16,8,128]{3,2,1,0:T(8,128)(2,1)S(1)}, bf16[2,16,8,128]{3,2,1,0:T(8,128)(2,1)S(1)}, u32[]{:S(2)}, u32[]{:S(2)}) collective-permute-start(bf16[2,16,8,128]{3,2,1,0:T(8,128)(2,1)S(1)} %maximum_maximum_fusion.3), channel_id=1, source_target_pairs={{1,0},{2,1},{3,2},{4,3},{5,4},{6,5},{7,6},{8,7},{9,8},{10,9},{11,1... | collective-permute-start | bytes 196616 | tf_op jit(solution)/shard_map/ppermute | solution.py:260
  67.2 9.5 %collective-permute-start.6 = (bf16[2,16,8,128]{3,2,1,0:T(8,128)(2,1)S(1)}, bf16[2,16,8,128]{3,2,1,0:T(8,128)(2,1)S(1)}, u32[]{:S(2)}, u32[]{:S(2)}) collective-permute-start(bf16[2,16,8,128]{3,2,1,0:T(8,128)(2,1)S(1)} %maximum_maximum_fusion.2), channel_id=1, source_target_pairs={{0,1},{1,2},{2,3},{3,4},{4,5},{5,6},{6,7},{7,8},{8,9},{9,10},{10,1... | collective-permute-start | bytes 196616 | tf_op jit(solution)/shard_map/ppermute | solution.py:260
  69.2 12.1 %collective-permute-start.10 = (bf16[2,64,8,128]{3,2,1,0:T(8,128)(2,1)S(1)}, bf16[2,64,8,128]{3,2,1,0:T(8,128)(2,1)S(1)}, u32[]{:S(2)}, u32[]{:S(2)}) collective-permute-start(bf16[2,64,8,128]{3,2,1,0:T(8,128)(2,1)S(1)} %pad_maximum_fusion.6), channel_id=1, source_target_pairs={{0,1},{1,2},{2,3},{3,4},{4,5},{5,6},{6,7},{7,8},{8,9},{9,10},{10,1... | collective-permute-start | bytes 786440 | tf_op jit(solution)/shard_map/ppermute | solution.py:260
  71.1 10.2 %collective-permute-start.11 = (bf16[2,64,8,128]{3,2,1,0:T(8,128)(2,1)S(1)}, bf16[2,64,8,128]{3,2,1,0:T(8,128)(2,1)S(1)}, u32[]{:S(2)}, u32[]{:S(2)}) collective-permute-start(bf16[2,64,8,128]{3,2,1,0:T(8,128)(2,1)S(1)} %pad_maximum_fusion.7), channel_id=1, source_target_pairs={{1,0},{2,1},{3,2},{4,3},{5,4},{6,5},{7,6},{8,7},{9,8},{10,9},{11,1... | collective-permute-start | bytes 786440 | tf_op jit(solution)/shard_map/ppermute | solution.py:260
  76.7 6.0 %collective-permute-start.8 = (bf16[2,8,80,128]{3,2,1,0:T(8,128)(2,1)S(1)}, bf16[2,8,80,128]{3,2,1,0:T(8,128)(2,1)S(1)}, u32[]{:S(2)}, u32[]{:S(2)}) collective-permute-start(bf16[2,8,80,128]{3,2,1,0:T(8,128)(2,1)S(1)} %pad_maximum_fusion.2), channel_id=1, source_target_pairs={{0,16},{16,32},{32,48},{48,64},{64,80},{80,96},{96,112},{112,128},... | collective-permute-start | bytes 983048 | tf_op jit(solution)/shard_map/ppermute | solution.py:260
  78.8 12.0 %collective-permute-start.9 = (bf16[2,8,80,128]{3,2,1,0:T(8,128)(2,1)S(1)}, bf16[2,8,80,128]{3,2,1,0:T(8,128)(2,1)S(1)}, u32[]{:S(2)}, u32[]{:S(2)}) collective-permute-start(bf16[2,8,80,128]{3,2,1,0:T(8,128)(2,1)S(1)} %pad_maximum_fusion.3), channel_id=1, source_target_pairs={{16,0},{32,16},{48,32},{64,48},{80,64},{96,80},{112,96},{128,112},... | collective-permute-start | bytes 983048 | tf_op jit(solution)/shard_map/ppermute | solution.py:260
